TPU v7x, 256 devices: a whole 4x4x8 slice. The times are simulated.
256 devices in a mesh: gx: 32 (over z, y), gy: 8 (over x, core).
Axes of the slice: x: 4, y: 4, z: 8, core: 2. Of those that a mesh axis runs over, the one named last changes fastest.
Arguments:
- image_feats: bfloat16 [65536, 4096], P('gx', 'gy'), may hold values from -6 to 6
- w_kv: bfloat16 [4096, 2048], P('gy'), may hold values from -0.09375 to 0.09375
- k_gain: float32 [128], replicated, may hold values from 0.25 to 1.75
- tile_rows: int32 [512], replicated, may hold values from 0 to 128
- deal: int32 [32, 16], replicated, may hold values from 0 to 511, as said below
Outputs:
- keys_out: bfloat16 [65536, 1024], P('gx', 'gy')
- values_out: bfloat16 [65536, 1024], P('gx', 'gy')
Inputs may be any that keep to these rules, and one draw needn't show every extreme that they name: Each input tile is named exactly once; deal[j, s] % 16 == s; two entries of one row j that name tiles of the same index of gx stand in columns s that differ by a multiple of 32, so one row names at most 1 tiles of one index of gx, and exactly 1 for some.
All inputs are finite; a program needn't handle non-finite values.
Results may differ from a plain program's by a relative error of at most 0.001.
Values may be sent and summed in bfloat16 or wider, within the bound.
A program may use at most 128 MiB of HBM per device.

v0:
```python
import jax
import jax.numpy as jnp
from jax import lax
from jax.sharding import PartitionSpec as P

HD = 128
TILE = 128
TPD = 16


epsilon = 1e-05


def local(image_feats, w_kv, k_gain, tile_rows, deal):
    local_width = image_feats.shape[1]
    groups = lax.axis_size("gx")
    own_index = lax.axis_index("gx")
    slots = max(1, TPD // groups)
    wanted = lax.dynamic_index_in_dim(deal, own_index, 0, keepdims=False)
    slot_index = jnp.arange(TPD, dtype=jnp.int32)
    slot_class = slot_index // groups
    places = jnp.arange(slots, dtype=jnp.int32)
    class_match = slot_class[None, :] == places[:, None]
    own_tiles = own_index * TPD + slot_index
    sending = deal == own_tiles[None, :]
    send_select = (sending[:, None, :] & class_match[None, :, :]).astype(jnp.bfloat16)
    blocks = image_feats.reshape(TPD, TILE, local_width)
    outgoing = jnp.einsum(
        "dcs,str->dctr", send_select, blocks, preferred_element_type=jnp.float32
    ).astype(jnp.bfloat16)
    incoming = lax.all_to_all(outgoing, "gx", split_axis=0, concat_axis=0, tiled=True)
    sources = jnp.arange(groups, dtype=jnp.int32)
    from_source = (wanted // TPD)[:, None] == sources[None, :]
    take_select = (from_source[:, :, None] & class_match.T[:, None, :]).astype(jnp.bfloat16)
    dealt_tiles = jnp.einsum(
        "snc,nctr->str", take_select, incoming, preferred_element_type=jnp.float32
    ).astype(jnp.bfloat16)
    row_count = TPD * TILE
    dealt_rows = dealt_tiles.reshape(row_count, local_width)
    total_kv = w_kv.shape[1] // 2
    partial_value = jnp.dot(dealt_rows, w_kv, preferred_element_type=jnp.float32)
    projected = lax.psum_scatter(
        partial_value.reshape(row_count, 2, total_kv), "gy", scatter_dimension=2, tiled=True
    )
    share_cols = projected.shape[2]
    key_pre = projected[:, 0, :].reshape(row_count, share_cols // HD, HD)
    value_pre = projected[:, 1, :]
    mean_square = jnp.mean(key_pre * key_pre, axis=-1, keepdims=True)
    normed = (key_pre * lax.rsqrt(mean_square + epsilon) * k_gain).reshape(row_count, share_cols)
    all_tiles = jnp.arange(tile_rows.shape[0], dtype=jnp.int32)
    limits = jnp.sum(
        jnp.where(wanted[:, None] == all_tiles[None, :], tile_rows[None, :], 0), axis=1
    )
    position = jnp.arange(TILE, dtype=jnp.int32)
    valid_rows = (position[None, :] < limits[:, None]).reshape(row_count, 1)
    keys_out = jnp.where(valid_rows, normed, 0.0).astype(jnp.bfloat16)
    values_out = jnp.where(valid_rows, value_pre, 0.0).astype(jnp.bfloat16)
    return (keys_out, values_out)


def solution(mesh):
    placed = (P("gx", "gy"), P("gy", None), P(), P(), P())
    return jax.shard_map(
        local, mesh=mesh, in_specs=placed, out_specs=(P("gx", "gy"), P("gx", "gy")), check_vma=False
    )
```

profile of v0, /device:TPU:1, one launch (start us, length us, event | category | flops | bytes accessed | tf_op | source)
XLA Modules:
  0.0 241.8 jit_solution(2279233354944163146)
XLA Ops:
  7.2 0.0 copy-start
  7.2 1.5 copy-done
  8.8 2.3 convert_bitcast_fusion
  11.1 4.4 %copy.18 = bf16[32,1,128,512]{3,2,1,0:T(8,128)(2,1)} copy(bf16[32,1,128,512]{3,0,2,1:T(8,128)(2,1)S(1)} %convert_bitcast_fusion) | data formatting | bytes 8388608 | tf_op jit(solution)/shard_map/convert_element_type | solution.py:30
  15.4 12.2 %all-to-all-start = ((bf16[32,1,128,512]{3,2,1,0:T(8,128)(2,1)}), bf16[32,1,128,512]{3,2,1,0:T(8,128)(2,1)}, u32[]{:S(2)}, u32[]{:S(2)}) async-start(bf16[32,1,128,512]{3,2,1,0:T(8,128)(2,1)} %copy.18), calls=%async_computation | async-start | bytes 8388608 | tf_op jit(solution)/shard_map/all_to_all | solution.py:31
  27.6 0.2 reduce-scatter.2.cloned.1.call-start
  27.8 0.0 copy-start.3
  27.8 3.9 %copy.22 = bf16[2048,512]{1,0:T(8,128)(2,1)} copy(bf16[2048,512]{0,1:T(8,128)(2,1)} %bitcast.34) | data formatting | bytes 4194304 | tf_op jit(solution)/shard_map/dot_general | solution.py:41
  31.7 0.0 copy-done.3
  31.7 0.2 dynamic-slice_reduce_fusion
  31.9 88.7 %all-to-all-done = bf16[32,1,128,512]{3,2,1,0:T(8,128)(2,1)} async-done(((bf16[32,1,128,512]{3,2,1,0:T(8,128)(2,1)}), bf16[32,1,128,512]{3,2,1,0:T(8,128)(2,1)}, u32[]{:S(2)}, u32[]{:S(2)}) %all-to-all-start) | async-done | bytes 4194336 | tf_op jit(solution)/shard_map/all_to_all | solution.py:31
  120.6 5.1 %fusion.4 = bf16[16,128,512]{2,0,1:T(8,128)(2,1)S(1)} fusion(bf16[32,1,128,512]{3,2,1,0:T(8,128)(2,1)} %all-to-all-done, s32[16]{0:T(128)S(1)} %and_select_fusion.1, pred[16]{0:T(512)(128)(4,1)S(1)} %fusion.21), kind=kOutput, calls=%fused_computation.5 | convolution fusion | flops 68158464 | bytes 6291536 | tf_op jit(solution)/shard_map/snc,nctr->str/dot_general | solution.py:35
  125.7 0.0 copy-start.2
  125.7 1.2 copy.20
  126.9 0.4 copy-done.2
  127.3 8.3 %fusion.22 = f32[2048,2,1024]{2,0,1:T(8,128)} fusion(bf16[2048,512,1]{1,0,2:T(8,128)(2,1)S(1)} %bitcast.36, bf16[2,1024,512]{2,1,0:T(8,128)(2,1)S(1)} %bitcast.35), kind=kOutput, calls=%fused_computation.38 | convolution fusion | flops 4294967296 | bytes 20971520 | tf_op jit(solution)/shard_map/dot_general | solution.py:41
  135.6 0.0 copy-start.4
  135.6 0.0 reduce-scatter.2.cloned.1.call-update
  135.6 0.7 copy-done.4
  136.2 0.0 copy-start.5
  136.2 0.2 select_reduce_fusion
  136.4 0.1 fusion.10
  136.5 93.0 %reduce-scatter.2.cloned.1.call-done = f32[2048,2,128]{2,0,1:T(8,128)} async-done(((f32[2048,2,1024]{2,0,1:T(8,128)}), f32[2048,2,128]{2,0,1:T(8,128)}) %reduce-scatter.2.cloned.1.call-update) | async-done | bytes 2097168 | tf_op jit(solution)/shard_map/reduce_scatter | solution.py:42
  229.5 0.0 copy-start.1
  229.5 1.7 multiply_reduce_fusion
  231.2 2.4 fusion.8
  233.6 0.0 copy-done.5
  233.6 0.0 copy-done.1
  233.6 1.4 fusion.9
  (4 shorter events, 0.0 us)
Async XLA Ops:
  7.2 1.6 copy-start
  15.4 105.2 %all-to-all-start = ((bf16[32,1,128,512]{3,2,1,0:T(8,128)(2,1)}), bf16[32,1,128,512]{3,2,1,0:T(8,128)(2,1)}, u32[]{:S(2)}, u32[]{:S(2)}) async-start(bf16[32,1,128,512]{3,2,1,0:T(8,128)(2,1)} %copy.18), calls=%async_computation | async-start | bytes 8388608 | tf_op jit(solution)/shard_map/all_to_all | solution.py:31
  27.6 201.9 %reduce-scatter.2.cloned.1.call-start = ((), (), s32[]{:S(2)}) async-start(), calls=%async_computation.2 | async-start | bytes 18874368 | tf_op jit(solution)/shard_map/reduce_scatter | solution.py:42
  27.8 3.9 %copy-start.3 = (s32[32,16]{0,1:T(8,128)S(1)}, s32[32,16]{0,1:T(8,128)}, u32[]{:S(2)}) copy-start(s32[32,16]{0,1:T(8,128)} %param.9) | copy-start | bytes 6148
  125.7 1.6 copy-start.2
  135.6 0.7 copy-start.4
  136.2 97.3 %copy-start.5 = (f32[128]{0:T(128)S(1)}, f32[128]{0:T(128)}, u32[]{:S(2)}) copy-start(f32[128]{0:T(128)} %param.7) | copy-start | bytes 1540
  229.5 4.1 %copy-start.1 = (f32[2048,2,128]{2,0,1:T(8,128)S(1)}, f32[2048,2,128]{2,0,1:T(8,128)}, u32[]{:S(2)}) copy-start(f32[2048,2,128]{2,0,1:T(8,128)} %reduce-scatter.2.cloned.1.call-done) | copy-start | bytes 6291460
Sparse Core Ops, SparseCore 0:
  135.7 93.7 reduce-scatter.1
where the time goes:
time: 242 us
  waiting for transfers between devices  182 us (75%)
  matrix products  15.6 us (6%)
  between operations  14.1 us (6%)
  starting transfers between devices  12.4 us (5%)
  local copies, waits for them, and re-layouts  12.3 us (5%)
  other arithmetic  5.75 us (2%)
    reduce_scatter x1, waiting for transfers between devices, local(): lax.psum_scatter(partial_value.reshape(row_count, 2, total_kv), 'gy', sca...  93 us
    all_to_all x1, waiting for transfers between devices, local(): lax.all_to_all(outgoing, 'gx', split_axis=0, concat_axis=0, tiled=True)  88.7 us
    all_to_all x1, starting transfers between devices, local(): lax.all_to_all(outgoing, 'gx', split_axis=0, concat_axis=0, tiled=True)  12.2 us
    dot_general x1, matrix products, local(): jnp.dot(dealt_rows, w_kv, preferred_element_type=jnp.float32)  8.28 us
    dot_general x1, matrix products, local(): jnp.einsum('snc,nctr->str', take_select, incoming, preferred_element_type...  5.05 us
  transfers between devices with their start and end apart: 2, of which 2 were waited for; matrix products, arithmetic and copies ran while one was open for 2% of the time, Pallas kernels for 0%

commit v1 on v0

v1 whole, which is shorter than its diff:
```python
import jax
import jax.numpy as jnp
from jax import lax
from jax.sharding import PartitionSpec as P

HD = 128
TILE = 128
TPD = 16


epsilon = 1e-05


def local(image_feats, w_kv, k_gain, tile_rows, deal):
    groups = lax.axis_size("gx")
    own_index = lax.axis_index("gx")
    slot_index = jnp.arange(TPD, dtype=jnp.int32)
    own_tiles = own_index * TPD + slot_index
    row_count = TPD * TILE
    total_kv = w_kv.shape[1] // 2
    partial_value = jnp.dot(image_feats, w_kv, preferred_element_type=jnp.float32)
    projected = lax.psum_scatter(
        partial_value.reshape(row_count, 2, total_kv), "gy", scatter_dimension=2, tiled=True
    )
    share = projected.shape[2]
    key_pre = projected[:, 0, :].reshape(row_count, share // HD, HD)
    value_pre = projected[:, 1, :]
    mean_square = jnp.mean(key_pre * key_pre, axis=-1, keepdims=True)
    normed = (key_pre * lax.rsqrt(mean_square + epsilon) * k_gain).reshape(row_count, share)
    limits = lax.dynamic_slice_in_dim(tile_rows, own_index * TPD, TPD)
    position = jnp.arange(TILE, dtype=jnp.int32)
    valid_rows = (position[None, :] < limits[:, None]).reshape(row_count, 1)
    keys = jnp.where(valid_rows, normed, 0.0).astype(jnp.bfloat16)
    values = jnp.where(valid_rows, value_pre, 0.0).astype(jnp.bfloat16)
    tiles = jnp.concatenate([keys, values], axis=1).reshape(TPD, TILE, 2 * share)
    sending = (deal == own_tiles[None, :]).astype(jnp.bfloat16)
    outgoing = jnp.einsum("ds,str->dtr", sending, tiles, preferred_element_type=jnp.float32).astype(jnp.bfloat16)
    incoming = lax.all_to_all(outgoing, "gx", split_axis=0, concat_axis=0, tiled=True)
    wanted = lax.dynamic_index_in_dim(deal, own_index, 0, keepdims=False)
    sources = jnp.arange(groups, dtype=jnp.int32)
    taking = ((wanted // TPD)[:, None] == sources[None, :]).astype(jnp.bfloat16)
    mine = jnp.einsum("sn,ntr->str", taking, incoming, preferred_element_type=jnp.float32).astype(jnp.bfloat16)
    mine = mine.reshape(row_count, 2 * share)
    return (mine[:, :share], mine[:, share:])


def solution(mesh):
    placed = (P("gx", "gy"), P("gy", None), P(), P(), P())
    return jax.shard_map(
        local, mesh=mesh, in_specs=placed, out_specs=(P("gx", "gy"), P("gx", "gy")), check_vma=False
    )
```

time: 242 us -> 215 us (0.89); the launches traced: 242 us -> 212 us
  waiting for transfers between devices: 182 us -> 145 us
  local copies, waits for them, and re-layouts: 12.3 us -> 24.4 us
  starting transfers between devices: 12.4 us -> 9.73 us
    all_to_all x1, waiting for transfers between devices: 88.7 us -> 47.8 us  [local(): lax.all_to_all(outgoing, 'gx', split_axis=0, concat_axis=0, tiled=True)]
    reshape x0 -> x1, local copies, waits for them, and re-layouts: none -> 18 us  [local(): partial_value.reshape(row_count, 2, total_kv)]
    reduce_scatter x1, waiting for transfers between devices: 93 us -> 96.9 us  [local(): lax.psum_scatter(partial_value.reshape(row_count, 2, total_kv), 'gy', sca...]
    dot_general x1 -> x0, local copies, waits for them, and re-layouts: 3.92 us -> none  [local(): jnp.dot(dealt_rows, w_kv, preferred_element_type=jnp.float32)]
    convert_element_type x2, local copies, waits for them, and re-layouts: 5.53 us -> 2.86 us  [the longest x1 2.5 us: local(): jnp.einsum('ds,str->dtr', sending, tiles, preferred_element_type=jnp.floa...]
    all_to_all x1, starting transfers between devices: 12.2 us -> 9.69 us  [local(): lax.all_to_all(outgoing, 'gx', split_axis=0, concat_axis=0, tiled=True)]
  transfers between devices with their start and end apart: 2 -> 2, of which waited for: 2 -> 2; matrix products, arithmetic and copies ran while one was open for 2% -> 0% of each run, Pallas kernels for 0% -> 0%
where the time goes in v1:
time: 215 us; the launch traced here: 212 us
  waiting for transfers between devices  145 us (67%)
  local copies, waits for them, and re-layouts  24.4 us (11%)
  between operations  14.1 us (7%)
  matrix products  13.4 us (6%)
  starting transfers between devices  9.73 us (5%)
  other arithmetic  5.88 us (3%)
    reduce_scatter x1, waiting for transfers between devices, local(): lax.psum_scatter(partial_value.reshape(row_count, 2, total_kv), 'gy', sca...  96.9 us
    all_to_all x1, waiting for transfers between devices, local(): lax.all_to_all(outgoing, 'gx', split_axis=0, concat_axis=0, tiled=True)  47.8 us
    reshape x1, local copies, waits for them, and re-layouts, local(): partial_value.reshape(row_count, 2, total_kv)  18 us
    dot_general x1, matrix products, local(): jnp.dot(image_feats, w_kv, preferred_element_type=jnp.float32)  9.79 us
    all_to_all x1, starting transfers between devices, local(): lax.all_to_all(outgoing, 'gx', split_axis=0, concat_axis=0, tiled=True)  9.69 us
  transfers between devices with their start and end apart: 2, of which 2 were waited for; matrix products, arithmetic and copies ran while one was open for 0% of the time, Pallas kernels for 0%

profile of v1, /device:TPU:1, one launch (start us, length us, event | category | flops | bytes accessed | tf_op | source)
XLA Modules:
  0.0 212.3 jit_solution(6918058758557024405)
XLA Ops:
  7.2 0.0 copy-start
  7.2 0.0 reduce-scatter.2.cloned.1.call-start
  7.2 1.5 copy-done
  8.8 9.8 %fusion.18 = f32[2048,2048]{0,1:T(8,128)} fusion(bf16[2048,512]{1,0:T(8,128)(2,1)S(1)} %copy-done, bf16[512,2048]{1,0:T(8,128)(2,1)} %param.6), kind=kOutput, calls=%fused_computation.29 | convolution fusion | flops 4294967296 | bytes 20971520 | tf_op jit(solution)/shard_map/dot_general | solution.py:21
  18.6 18.0 %copy.11 = f32[2048,2,1024]{2,0,1:T(8,128)} copy(f32[2048,2,1024]{0,2,1:T(8,128)} %bitcast.12) | data formatting | bytes 33554432 | tf_op jit(solution)/shard_map/reshape | solution.py:23
  36.5 0.0 copy-start.2
  36.5 0.0 reduce-scatter.2.cloned.1.call-update
  36.6 0.8 dynamic_slice.8
  37.3 96.9 %reduce-scatter.2.cloned.1.call-done = f32[2048,2,128]{2,0,1:T(8,128)} async-done(((f32[2048,2,1024]{2,0,1:T(8,128)}), f32[2048,2,128]{2,0,1:T(8,128)}) %reduce-scatter.2.cloned.1.call-update) | async-done | bytes 2097168 | tf_op jit(solution)/shard_map/reduce_scatter | solution.py:22
  134.3 1.6 multiply_reduce_fusion
  135.9 0.0 copy-done.2
  135.9 0.0 copy-start.1
  135.9 1.9 multiply_multiply_fusion
  137.8 2.4 %fusion.9 = (bf16[16,128,128]{2,0,1:T(8,128)(2,1)S(1)}, bf16[16,128,128]{2,0,1:T(8,128)(2,1)S(1)}) fusion(bf16[16,128,128]{2,1,0:T(8,128)(2,1)S(1)} %bitcast.14, pred[16,128]{0,1:T(8,128)(4,1)S(1)} %iota_compare_fusion, bf16[16,128,128]{2,1,0:T(8,128)(2,1)S(1)} %bitcast.15), kind=kLoop, calls=%fused_computation.10 | loop fusion | flops 524288 | bytes 2099200 | tf_op jit(solution)/shard_map/convert_element_type | solution.py:33
  140.2 0.0 copy-done.1
  140.2 0.8 convolution_convert_fusion
  141.0 2.5 %copy.14 = bf16[32,128,256]{2,1,0:T(8,128)(2,1)} copy(bf16[32,128,256]{2,0,1:T(8,128)(2,1)S(1)} %convolution_convert_fusion) | data formatting | bytes 4194304 | tf_op jit(solution)/shard_map/convert_element_type | solution.py:37
  143.5 9.7 %all-to-all-start = ((bf16[32,128,256]{2,1,0:T(8,128)(2,1)}), bf16[32,128,256]{2,1,0:T(8,128)(2,1)}, u32[]{:S(2)}, u32[]{:S(2)}) async-start(bf16[32,128,256]{2,1,0:T(8,128)(2,1)} %copy.14), calls=%async_computation.1 | async-start | bytes 4194304 | tf_op jit(solution)/shard_map/all_to_all | solution.py:38
  153.2 0.2 dynamic-slice_reduce_fusion
  153.4 47.8 %all-to-all-done = bf16[32,128,256]{2,1,0:T(8,128)(2,1)} async-done(((bf16[32,128,256]{2,1,0:T(8,128)(2,1)}), bf16[32,128,256]{2,1,0:T(8,128)(2,1)}, u32[]{:S(2)}, u32[]{:S(2)}) %all-to-all-start) | async-done | bytes 2097184 | tf_op jit(solution)/shard_map/all_to_all | solution.py:38
  201.2 2.8 %fusion.2 = bf16[16,128,256]{2,0,1:T(8,128)(2,1)S(1)} fusion(bf16[32,128,256]{2,1,0:T(8,128)(2,1)} %all-to-all-done, s32[16]{0:T(128)S(1)} %and_select_fusion), kind=kOutput, calls=%fused_computation.3 | convolution fusion | flops 34079232 | bytes 3145792 | tf_op jit(solution)/shard_map/sn,ntr->str/dot_general | solution.py:42
  204.0 0.4 copy.16
  204.4 1.0 fusion.17
  (4 shorter events, 0.0 us)
Async XLA Ops:
  7.2 1.6 copy-start
  7.2 127.1 %reduce-scatter.2.cloned.1.call-start = ((), (), s32[]{:S(2)}) async-start(), calls=%async_computation.2 | async-start | bytes 18874368 | tf_op jit(solution)/shard_map/reduce_scatter | solution.py:22
  36.5 99.3 %copy-start.2 = (f32[128]{0:T(128)S(1)}, f32[128]{0:T(128)}, u32[]{:S(2)}) copy-start(f32[128]{0:T(128)} %param.7) | copy-start | bytes 1540
  135.9 4.3 %copy-start.1 = (s32[32,16]{0,1:T(8,128)S(1)}, s32[32,16]{0,1:T(8,128)}, u32[]{:S(2)}) copy-start(s32[32,16]{0,1:T(8,128)} %param.9) | copy-start | bytes 6148
  143.5 57.7 %all-to-all-start = ((bf16[32,128,256]{2,1,0:T(8,128)(2,1)}), bf16[32,128,256]{2,1,0:T(8,128)(2,1)}, u32[]{:S(2)}, u32[]{:S(2)}) async-start(bf16[32,128,256]{2,1,0:T(8,128)(2,1)} %copy.14), calls=%async_computation.1 | async-start | bytes 4194304 | tf_op jit(solution)/shard_map/all_to_all | solution.py:38
Sparse Core Ops, SparseCore 0:
  36.7 97.5 reduce-scatter.1

commit v2 on v1

v2 whole, which is shorter than its diff:
```python
import functools

import jax
import jax.numpy as jnp
from jax import lax
from jax.experimental import pallas as pl
from jax.experimental.pallas import tpu as pltpu
from jax.sharding import PartitionSpec as P

HD = 128
EPSILON = 1e-05
CHUNKS = 8
MESH = pl.DeviceIdType.MESH


def offsets(nz, ny):
    pairs = [(dz, dy) for dz in range(nz) for dy in range(ny) if (dz, dy) != (0, 0)]
    near = lambda d, n: min(d, n - d)
    return sorted(pairs, key=lambda p: (-near(p[0], nz) - near(p[1], ny), p[0], p[1]))


def kernel(
    nz, ny, tpd, tile, chunks,
    x_ref, w_ref, gain_ref, rows_ref, deal_ref, k_ref, v_ref,
    wv, xo, xr, keep, ps, pr, rs, rr, tiles, sb, rb, table,
    w_local, w_send, w_recv, x_local, x_send, x_recv,
    p_send, p_recv, r_send, r_recv, d_send, d_recv,
):
    groups = nz * ny
    rows = tile // chunks
    feats = x_ref.shape[2]
    total_kv = w_ref.shape[1] // 2
    gx, gy = lax.axis_index("gx"), lax.axis_index("gy")
    z, y = gx // ny, lax.rem(gx, ny)
    chip, core = gy // 2, lax.rem(gy, 2)
    mate = chip + 1 - 2 * lax.rem(chip, 2)
    across = 3 - chip
    sibling_id = (gx, chip * 2 + 1 - core)
    mate_id = (gx, mate * 2 + core)
    across_id = (gx, across * 2 + core)

    def owners(which, its_core):
        return (
            which * 2 + its_core, (3 - which) * 2 + its_core,
            which * 2 + 1 - its_core, (3 - which) * 2 + 1 - its_core,
        )

    def columns(owner, part):
        return pl.ds(pl.multiple_of(owner * HD + part * total_kv, HD), HD)

    def peer(dz, dy):
        return lax.rem(z + dz, nz) * ny + lax.rem(y + dy, ny)

    def remote(src, dst, send, recv, device):
        return pltpu.make_async_remote_copy(
            src_ref=src, dst_ref=dst, send_sem=send, recv_sem=recv, device_id=device, device_id_type=MESH
        )

    for block, owner in enumerate(owners(chip, core)):
        for part in range(2):
            pltpu.make_async_copy(
                w_ref.at[:, columns(owner, part)],
                wv.at[pl.ds(0, feats), pl.ds((2 * block + part) * HD, HD)],
                w_local,
            ).start()
    for q in range(chunks):
        pltpu.make_async_copy(x_ref.at[:, pl.ds(q * rows, rows), :], xo.at[q], x_local.at[q]).start()

    barrier = pltpu.get_barrier_semaphore()
    spread = offsets(nz, ny)
    for device in (sibling_id, mate_id, across_id):
        pl.semaphore_signal(barrier, inc=1, device_id=device, device_id_type=MESH)
    for dz, dy in spread:
        pl.semaphore_signal(barrier, inc=1, device_id=(peer(dz, dy), gy), device_id_type=MESH)
    pl.semaphore_wait(barrier, 3 + len(spread))

    for block, owner in enumerate(owners(mate, core)):
        for part in range(2):
            remote(
                w_ref.at[:, columns(owner, part)],
                wv.at[pl.ds(feats, feats), pl.ds((2 * block + part) * HD, HD)],
                w_send, w_recv, mate_id,
            ).start()
    for q in range(chunks):
        remote(x_ref.at[:, pl.ds(q * rows, rows), :], xr.at[q], x_send, x_recv.at[q], mate_id).start()

    def find(d, carry):
        found = jnp.int32(0)
        for s in range(tpd):
            source = lax.div(deal_ref[d * tpd + s], jnp.int32(tpd))
            found = jnp.where(source == gx, s, found)
        table[d] = found
        return carry

    lax.fori_loop(0, groups, find, 0)

    pltpu.make_async_copy(w_ref.at[:, pl.ds(0, 8 * HD)], wv.at[pl.ds(0, feats), :], w_local).wait()
    remote(wv.at[pl.ds(0, feats), :], wv.at[pl.ds(feats, feats), :], w_send, w_recv, mate_id).wait_recv()

    count = tpd * rows
    half = 4 * HD

    def project(q):
        pltpu.make_async_copy(x_ref.at[:, pl.ds(0, rows), :], xo.at[q], x_local.at[q]).wait()
        remote(xo.at[q], xr.at[q], x_send, x_recv.at[q], mate_id).wait_recv()
        own = xo[q].reshape(count, feats)
        other = xr[q].reshape(count, feats)
        for part, ref in ((1, ps), (0, keep)):
            ref[q] = jnp.dot(
                own, wv[0:feats, part * half:(part + 1) * half], preferred_element_type=jnp.float32
            ) + jnp.dot(
                other, wv[feats:2 * feats, part * half:(part + 1) * half], preferred_element_type=jnp.float32
            )
            if part:
                remote(ps.at[q], pr.at[q], p_send, p_recv.at[q], sibling_id).start()
        remote(ps.at[q], pr.at[q], p_send, p_recv.at[q], sibling_id).wait_recv()
        rs[q] = keep[q, :, 2 * HD:] + pr[q, :, 2 * HD:]
        remote(rs.at[q], rr.at[q], r_send, r_recv.at[q], across_id).start()
        keep[q, :, :2 * HD] = keep[q, :, :2 * HD] + pr[q, :, :2 * HD]

    def finish(q):
        remote(rs.at[q], rr.at[q], r_send, r_recv.at[q], across_id).wait_recv()
        gain = gain_ref[...]
        for s in range(tpd):
            span = pl.ds(s * rows, rows)
            key_pre = keep[q, span, :HD] + rr[q, span, :HD]
            value_pre = keep[q, span, HD:2 * HD] + rr[q, span, HD:]
            mean_square = jnp.mean(key_pre * key_pre, axis=-1, keepdims=True)
            normed = key_pre * lax.rsqrt(mean_square + EPSILON) * gain
            position = lax.broadcasted_iota(jnp.int32, (rows, HD), 0) + q * rows
            valid = position < rows_ref[gx * tpd + s]
            tiles[s, :, :HD] = jnp.where(valid, normed, 0.0).astype(jnp.bfloat16)
            tiles[s, :, HD:] = jnp.where(valid, value_pre, 0.0).astype(jnp.bfloat16)

        def fill(d, carry):
            sb[q, d] = tiles[table[d]]
            return carry

        lax.fori_loop(0, groups, fill, 0)
        place = pl.ds(pl.multiple_of(q * rows, rows), rows)
        rb[gx, place, :] = tiles[table[gx]]
        for dz, dy in spread:
            target = peer(dz, dy)
            remote(sb.at[q, target], rb.at[gx, place, :], d_send, d_recv, (target, gy)).start()

    def step(i, carry):
        @pl.when(i < chunks)
        def _():
            project(i)

        @pl.when(i >= 1)
        def _():
            finish(i - 1)

        return carry

    lax.fori_loop(0, chunks + 1, step, 0)

    far = peer(*spread[0])
    remote(sb.at[:, pl.ds(0, groups - 1)], rb.at[pl.ds(0, groups - 1)], d_send, d_recv, (far, gy)).wait_recv()
    for s in range(tpd):
        source = lax.div(deal_ref[gx * tpd + s], jnp.int32(tpd))
        k_ref[s] = rb[source, :, :HD]
        v_ref[s] = rb[source, :, HD:]

    remote(wv.at[pl.ds(0, feats), :], wv.at[pl.ds(feats, feats), :], w_send, w_recv, mate_id).wait_send()
    remote(xo, xr, x_send, x_recv.at[0], mate_id).wait_send()
    remote(ps, pr, p_send, p_recv.at[0], sibling_id).wait_send()
    remote(rs, rr, r_send, r_recv.at[0], across_id).wait_send()
    remote(sb.at[:, pl.ds(0, groups - 1)], rb.at[pl.ds(0, groups - 1)], d_send, d_recv, (far, gy)).wait_send()


def local(nz, ny, tpd, tile, chunks, image_feats, w_kv, k_gain, tile_rows, deal):
    feats = image_feats.shape[1]
    groups = nz * ny
    rows = tile // chunks
    count = tpd * rows
    bf16, f32 = jnp.bfloat16, jnp.float32
    dma = pltpu.SemaphoreType.DMA
    any_space = pl.BlockSpec(memory_space=pltpu.HBM)
    vmem = pl.BlockSpec(memory_space=pltpu.VMEM)
    smem = pl.BlockSpec(memory_space=pltpu.SMEM)
    keys, values = pl.pallas_call(
        functools.partial(kernel, nz, ny, tpd, tile, chunks),
        out_shape=(jax.ShapeDtypeStruct((tpd, tile, HD), bf16),) * 2,
        in_specs=[any_space, any_space, vmem, smem, smem],
        out_specs=(vmem, vmem),
        scratch_shapes=[
            pltpu.VMEM((2 * feats, 8 * HD), bf16),
            pltpu.VMEM((chunks, tpd, rows, feats), bf16),
            pltpu.VMEM((chunks, tpd, rows, feats), bf16),
            pltpu.VMEM((chunks, count, 4 * HD), f32),
            pltpu.VMEM((chunks, count, 4 * HD), f32),
            pltpu.VMEM((chunks, count, 4 * HD), f32),
            pltpu.VMEM((chunks, count, 2 * HD), f32),
            pltpu.VMEM((chunks, count, 2 * HD), f32),
            pltpu.VMEM((tpd, rows, 2 * HD), bf16),
            pltpu.VMEM((chunks, groups, rows, 2 * HD), bf16),
            pltpu.VMEM((groups, tile, 2 * HD), bf16),
            pltpu.SMEM((groups,), jnp.int32),
            dma, dma, dma, dma((chunks,)), dma, dma((chunks,)),
            dma, dma((chunks,)), dma, dma((chunks,)), dma, dma,
        ],
        compiler_params=pltpu.CompilerParams(
            collective_id=0, has_side_effects=True, vmem_limit_bytes=63 * 1024 * 1024
        ),
    )(
        image_feats.reshape(tpd, tile, feats), w_kv, k_gain.reshape(1, HD),
        tile_rows, deal.reshape(-1),
    )
    return (keys.reshape(tpd * tile, HD), values.reshape(tpd * tile, HD))


def build(mesh, nz, ny, tpd, tile, chunks):
    placed = (P("gx", "gy"), P("gy", None), P(), P(), P())
    return jax.shard_map(
        functools.partial(local, nz, ny, tpd, tile, chunks),
        mesh=mesh, in_specs=placed, out_specs=(P("gx", "gy"), P("gx", "gy")), check_vma=False,
    )


def solution(mesh):
    return build(mesh, 8, 4, 16, 128, CHUNKS)
```

time: 215 us -> 108 us (0.50)
  waiting for transfers between devices: 145 us -> 0 us
  Pallas kernels: 0 us -> 102 us
  local copies, waits for them, and re-layouts: 24.4 us -> 5.17 us
  between operations: 14.1 us -> 0.64 us
  matrix products: 13.4 us -> 0 us
  starting transfers between devices: 9.73 us -> 0 us
  other arithmetic: 5.88 us -> 0 us
    pallas_call x0 -> x1, Pallas kernels: none -> 102 us  [local(): pl.pallas_call(functools.partial(kernel, nz, ny, tpd, tile, chunks), out_...]
    reduce_scatter x1 -> x0, waiting for transfers between devices: 96.9 us -> none  [local(): lax.psum_scatter(partial_value.reshape(row_count, 2, total_kv), 'gy', sca...]
    all_to_all x1 -> x0, waiting for transfers between devices: 47.8 us -> none  [local(): lax.all_to_all(outgoing, 'gx', split_axis=0, concat_axis=0, tiled=True)]
    reshape x1, local copies, waits for them, and re-layouts: 18 us -> 0.66 us  [local(): deal.reshape(-1)]
    dot_general x3 -> x0, matrix products: 13.4 us -> none  [the longest x1 9.79 us: local(): jnp.dot(image_feats, w_kv, preferred_element_type=jnp.float32)]
    all_to_all x1 -> x0, starting transfers between devices: 9.69 us -> none  [local(): lax.all_to_all(outgoing, 'gx', split_axis=0, concat_axis=0, tiled=True)]
    unnamed x6 -> x3, local copies, waits for them, and re-layouts: 1.55 us -> 4.51 us
    convert_element_type x2 -> x0, local copies, waits for them, and re-layouts: 2.86 us -> none  [the longest x1 2.5 us: local(): jnp.einsum('ds,str->dtr', sending, tiles, preferred_element_type=jnp.floa...]
  transfers between devices with their start and end apart: 2 -> 0, of which waited for: 2 -> 0; matrix products, arithmetic and copies ran while one was open for 0% -> 0% of each run, Pallas kernels for 0% -> 0%
where the time goes in v2:
time: 108 us; the launch traced here: 107 us
  Pallas kernels  102 us (94%)
  local copies, waits for them, and re-layouts  5.17 us (5%)
    pallas_call x1, Pallas kernels, local(): pl.pallas_call(functools.partial(kernel, nz, ny, tpd, tile, chunks), out_...  102 us
    unnamed x3, local copies, waits for them, and re-layouts  4.51 us

profile of v2, /device:TPU:1, one launch (start us, length us, event | category | flops | bytes accessed | tf_op | source)
XLA Modules:
  0.0 107.4 jit_solution(1161781754910655066)
XLA Ops:
  0.6 0.8 copy.7
  1.4 0.7 reshape.21.deal_ref
  2.1 101.6 %shard_map.68 = (bf16[16,128,128]{2,1,0:T(8,128)(2,1)}, bf16[16,128,128]{2,1,0:T(8,128)(2,1)}) custom-call(bf16[16,128,512]{2,1,0:T(8,128)(2,1)} %bitcast.4, bf16[512,2048]{1,0:T(8,128)(2,1)} %w_ref.1, f32[1,128]{1,0:T(1,128)} %bitcast.7, s32[512]{0:T(512)} %rows_ref.1, s32[512]{0:T(512)} %reshape.21.deal_ref), custom_call_target="tpu_custom_call" | custom-call | tf_op jit(solution)/shard_map/pallas_call | solution.py:183
  103.7 1.9 %copy.10 = bf16[2048,128]{1,0:T(8,128)(2,1)} copy(bf16[2048,128]{1,0:T(8,128)(2,1)} %bitcast.6) | data formatting | bytes 1048576
  105.5 1.9 %copy.11 = bf16[2048,128]{1,0:T(8,128)(2,1)} copy(bf16[2048,128]{1,0:T(8,128)(2,1)} %bitcast.5) | data formatting | bytes 1048576

commit v3 on v2

v3 whole, which is shorter than its diff:
```python
import functools

import jax
import jax.numpy as jnp
from jax import lax
from jax.experimental import pallas as pl
from jax.experimental.pallas import tpu as pltpu
from jax.sharding import PartitionSpec as P

HD = 128
EPSILON = 1e-05
CHUNKS = 8
EARLY = 2
LAG = 2
MESH = pl.DeviceIdType.MESH


def offsets(nz, ny):
    pairs = [(dz, dy) for dz in range(nz) for dy in range(ny) if (dz, dy) != (0, 0)]
    near = lambda d, n: min(d, n - d)
    return sorted(pairs, key=lambda p: (-near(p[0], nz) - near(p[1], ny), p[0], p[1]))


def kernel(
    nz, ny, tpd, tile, chunks, early,
    x_ref, w_ref, gain_ref, rows_ref, deal_ref, k_ref, v_ref,
    wv, xo, xr, xf, xs, xd, keep, ps, pr, rs, rr, tiles, sb, rb, table,
    w_local, w_send, w_mate, w_near, w_far, x_local, x_send, x_recv, f_local, f_send, f_recv,
    p_send, p_recv, r_send, r_recv, d_send, d_recv,
):
    groups = nz * ny
    rows = tile // chunks
    late = chunks - early
    late_rows, early_rows = late * rows, early * rows
    feats = x_ref.shape[2]
    total_kv = w_ref.shape[1] // 2
    tpu = tpd // 2
    count = tpu * rows
    units = 2 * chunks
    late_units = 2 * late
    gx, gy = lax.axis_index("gx"), lax.axis_index("gy")
    z, y = gx // ny, lax.rem(gx, ny)
    chip, core = gy // 2, lax.rem(gy, 2)
    mate = chip + 1 - 2 * lax.rem(chip, 2)
    across = 3 - chip
    sibling_id = (gx, chip * 2 + 1 - core)
    mate_id = (gx, mate * 2 + core)
    across_id = (gx, across * 2 + core)

    def owners(which, its_core):
        return (
            which * 2 + its_core, (3 - which) * 2 + its_core,
            which * 2 + 1 - its_core, (3 - which) * 2 + 1 - its_core,
        )

    def columns(owner, part):
        return pl.ds(pl.multiple_of(owner * HD + part * total_kv, HD), HD)

    def peer(dz, dy):
        return lax.rem(z + dz, nz) * ny + lax.rem(y + dy, ny)

    def remote(src, dst, send, recv, device):
        return pltpu.make_async_remote_copy(
            src_ref=src, dst_ref=dst, send_sem=send, recv_sem=recv, device_id=device, device_id_type=MESH
        )

    for block, owner in enumerate(owners(chip, core)):
        for part in range(2):
            pltpu.make_async_copy(
                w_ref.at[:, columns(owner, part)],
                wv.at[pl.ds(0, feats), pl.ds((2 * block + part) * HD, HD)],
                w_local,
            ).start()
    pltpu.make_async_copy(x_ref.at[:, pl.ds(late_rows, early_rows), :], xf, f_local).start()
    for u in range(late_units):
        pltpu.make_async_copy(
            x_ref.at[pl.ds(u % 2 * tpu, tpu), pl.ds(u // 2 * rows, rows), :], xo.at[u], x_local.at[u]
        ).start()

    barrier = pltpu.get_barrier_semaphore()
    spread = offsets(nz, ny)
    for device in (sibling_id, mate_id, across_id):
        pl.semaphore_signal(barrier, inc=1, device_id=device, device_id_type=MESH)
    for dz, dy in spread:
        pl.semaphore_signal(barrier, inc=1, device_id=(peer(dz, dy), gy), device_id_type=MESH)

    def find(d, carry):
        found = jnp.int32(0)
        for s in range(tpd):
            source = lax.div(deal_ref[s, d], jnp.int32(tpd))
            found = jnp.where(source == gx, s, found)
        table[d] = found
        return carry

    lax.fori_loop(0, groups, find, 0)
    pltpu.make_async_copy(x_ref.at[:, pl.ds(late_rows, early_rows), :], xf, f_local).wait()

    def gather(d, carry):
        xs[d] = xf[table[d]]
        return carry

    lax.fori_loop(0, groups, gather, 0)
    xd[gx] = xf[table[gx]]
    pl.semaphore_wait(barrier, 3 + len(spread))

    quarter = feats // ny
    part_rows = quarter // 2

    def share(owner_y, half):
        at = pl.multiple_of(feats + owner_y * quarter + half * part_rows, part_rows)
        return wv.at[pl.ds(at, part_rows), :]

    for half in range(2):
        source = pl.ds(pl.multiple_of(y * quarter + half * part_rows, part_rows), part_rows)
        at = pl.ds(pl.multiple_of(feats + y * quarter + half * part_rows, part_rows), part_rows)
        for block, owner in enumerate(owners(mate, core)):
            for part in range(2):
                remote(
                    w_ref.at[source, columns(owner, part)],
                    wv.at[at, pl.ds((2 * block + part) * HD, HD)],
                    w_send, w_mate.at[half], mate_id,
                ).start()
    for u in range(late_units):
        remote(
            x_ref.at[pl.ds(u % 2 * tpu, tpu), pl.ds(u // 2 * rows, rows), :],
            xr.at[u], x_send, x_recv.at[u], mate_id,
        ).start()
    for dz, dy in spread:
        if dy == 0:
            target = peer(dz, dy)
            remote(xs.at[target], xd.at[gx], f_send, f_recv, (target, gy)).start()

    up, down = lax.rem(y + 1, ny), lax.rem(y + ny - 1, ny)
    up_id, down_id = (z * ny + up, gy), (z * ny + down, gy)
    for half in range(2):
        remote(share(y, half), share(y, half), w_send, w_mate.at[half], mate_id).wait_recv()
        remote(share(y, half), share(y, half), w_send, w_near.at[0, half], up_id).start()
        remote(share(y, half), share(y, half), w_send, w_near.at[1, half], down_id).start()
    remote(share(down, 0), share(down, 0), w_send, w_near.at[0, 0], up_id).wait_recv()
    remote(share(down, 0), share(down, 0), w_send, w_far.at[0], up_id).start()
    remote(share(up, 1), share(up, 1), w_send, w_near.at[1, 1], down_id).wait_recv()
    remote(share(up, 1), share(up, 1), w_send, w_far.at[1], down_id).start()
    for dz, dy in spread:
        if dy != 0:
            target = peer(dz, dy)
            remote(xs.at[target], xd.at[gx], f_send, f_recv, (target, gy)).start()
    opposite = lax.rem(y + 2, ny)
    remote(share(up, 0), share(up, 0), w_send, w_near.at[1, 0], down_id).wait_recv()
    remote(share(down, 1), share(down, 1), w_send, w_near.at[0, 1], up_id).wait_recv()
    remote(share(opposite, 0), share(opposite, 0), w_send, w_far.at[0], up_id).wait_recv()
    remote(share(opposite, 1), share(opposite, 1), w_send, w_far.at[1], down_id).wait_recv()
    pltpu.make_async_copy(w_ref.at[:, pl.ds(0, 8 * HD)], wv.at[pl.ds(0, feats), :], w_local).wait()

    far = peer(*spread[0])
    half_cols = 4 * HD

    def project(u):
        @pl.when(u < late_units)
        def _():
            pltpu.make_async_copy(x_ref.at[pl.ds(0, tpu), pl.ds(0, rows), :], xo.at[u], x_local.at[u]).wait()

        remote(xo.at[u], xr.at[u], x_send, x_recv.at[u], mate_id).wait_recv()
        own = xo[u].reshape(count, feats)
        other = xr[u].reshape(count, feats)
        for part, ref in ((1, ps), (0, keep)):
            ref[u] = jnp.dot(
                own, wv[0:feats, part * half_cols:(part + 1) * half_cols], preferred_element_type=jnp.float32
            ) + jnp.dot(
                other, wv[feats:2 * feats, part * half_cols:(part + 1) * half_cols],
                preferred_element_type=jnp.float32,
            )
            if part:
                remote(ps.at[u], pr.at[u], p_send, p_recv.at[u], sibling_id).start()
        remote(ps.at[u], pr.at[u], p_send, p_recv.at[u], sibling_id).wait_recv()
        rs[u] = keep[u, :, 2 * HD:] + pr[u, :, 2 * HD:]
        remote(rs.at[u], rr.at[u], r_send, r_recv.at[u], across_id).start()
        keep[u, :, :2 * HD] = keep[u, :, :2 * HD] + pr[u, :, :2 * HD]

    def normalize(u, store):
        q, h = lax.div(u, 2), lax.rem(u, 2)
        remote(rs.at[u], rr.at[u], r_send, r_recv.at[u], across_id).wait_recv()
        gain = gain_ref[...]
        for s in range(tpu):
            span = pl.ds(s * rows, rows)
            key_pre = keep[u, span, :HD] + rr[u, span, :HD]
            value_pre = keep[u, span, HD:2 * HD] + rr[u, span, HD:]
            mean_square = jnp.mean(key_pre * key_pre, axis=-1, keepdims=True)
            normed = key_pre * lax.rsqrt(mean_square + EPSILON) * gain
            position = lax.broadcasted_iota(jnp.int32, (rows, HD), 0) + q * rows
            store(h * tpu + s, position, normed, value_pre)

    def finish_late(u):
        q = lax.div(u, 2)

        def store(s, position, normed, value_pre):
            valid = position < rows_ref[gx * tpd + s]
            tiles[s, :, :HD] = jnp.where(valid, normed, 0.0).astype(jnp.bfloat16)
            tiles[s, :, HD:] = jnp.where(valid, value_pre, 0.0).astype(jnp.bfloat16)

        normalize(u, store)

        @pl.when(lax.rem(u, 2) == 1)
        def _():
            def fill(d, carry):
                sb[q, d] = tiles[table[d]]
                return carry

            lax.fori_loop(0, groups, fill, 0)
            place = pl.ds(pl.multiple_of(q * rows, rows), rows)
            rb[gx, place, :] = tiles[table[gx]]
            for dz, dy in spread:
                target = peer(dz, dy)
                remote(sb.at[q, target], rb.at[gx, place, :], d_send, d_recv, (target, gy)).start()

    def finish_early(u):
        place = pl.ds(pl.multiple_of(lax.div(u, 2) * rows, rows), rows)

        def store(s, position, normed, value_pre):
            valid = position < rows_ref[deal_ref[s, gx]]
            k_ref[s, place, :] = jnp.where(valid, normed, 0.0).astype(jnp.bfloat16)
            v_ref[s, place, :] = jnp.where(valid, value_pre, 0.0).astype(jnp.bfloat16)

        normalize(u, store)

    def take_early():
        remote(xs.at[pl.ds(0, groups - 1)], xd.at[pl.ds(0, groups - 1)], f_send, f_recv, (far, gy)).wait_recv()
        for s in range(tpd):
            source = lax.div(deal_ref[s, gx], jnp.int32(tpd))
            for e in range(early):
                xo[late_units + 2 * e + s // tpu, s % tpu] = xd[source, e * rows:(e + 1) * rows, :]
        for u in range(late_units, units):
            remote(xo.at[u], xr.at[u], x_send, x_recv.at[u], mate_id).start()

    def step(i, carry):
        @pl.when(i < units)
        def _():
            project(i)

        @pl.when(i == max(late_units - 3, 0))
        def _():
            take_early()

        @pl.when((i >= LAG) & (i < late_units + LAG))
        def _():
            finish_late(i - LAG)

        @pl.when(i >= late_units + LAG)
        def _():
            finish_early(i - LAG)

        return carry

    lax.fori_loop(0, units + LAG, step, 0)

    remote(sb.at[:, pl.ds(0, groups - 1)], rb.at[pl.ds(0, groups - 1)], d_send, d_recv, (far, gy)).wait_recv()
    for s in range(tpd):
        source = lax.div(deal_ref[s, gx], jnp.int32(tpd))
        k_ref[s, 0:late_rows, :] = rb[source, :, :HD]
        v_ref[s, 0:late_rows, :] = rb[source, :, HD:]

    remote(wv.at[pl.ds(0, feats), :], wv.at[pl.ds(0, feats), :], w_send, w_mate.at[0], mate_id).wait_send()
    remote(xo, xr, x_send, x_recv.at[0], mate_id).wait_send()
    remote(xs.at[pl.ds(0, groups - 1)], xd.at[pl.ds(0, groups - 1)], f_send, f_recv, (far, gy)).wait_send()
    remote(ps, pr, p_send, p_recv.at[0], sibling_id).wait_send()
    remote(rs, rr, r_send, r_recv.at[0], across_id).wait_send()
    remote(sb.at[:, pl.ds(0, groups - 1)], rb.at[pl.ds(0, groups - 1)], d_send, d_recv, (far, gy)).wait_send()


def local(nz, ny, tpd, tile, chunks, early, image_feats, w_kv, k_gain, tile_rows, deal):
    feats = image_feats.shape[1]
    groups = nz * ny
    rows = tile // chunks
    units = 2 * chunks
    late = chunks - early
    count = tpd // 2 * rows
    bf16, f32 = jnp.bfloat16, jnp.float32
    dma = pltpu.SemaphoreType.DMA
    any_space = pl.BlockSpec(memory_space=pltpu.HBM)
    vmem = pl.BlockSpec(memory_space=pltpu.VMEM)
    smem = pl.BlockSpec(memory_space=pltpu.SMEM)
    keys, values = pl.pallas_call(
        functools.partial(kernel, nz, ny, tpd, tile, chunks, early),
        out_shape=(jax.ShapeDtypeStruct((tpd, tile, HD), bf16),) * 2,
        in_specs=[any_space, any_space, vmem, smem, smem],
        out_specs=(vmem, vmem),
        scratch_shapes=[
            pltpu.VMEM((2 * feats, 8 * HD), bf16),
            pltpu.VMEM((units, tpd // 2, rows, feats), bf16),
            pltpu.VMEM((units, tpd // 2, rows, feats), bf16),
            pltpu.VMEM((tpd, early * rows, feats), bf16),
            pltpu.VMEM((groups, early * rows, feats), bf16),
            pltpu.VMEM((groups, early * rows, feats), bf16),
            pltpu.VMEM((units, count, 4 * HD), f32),
            pltpu.VMEM((units, count, 4 * HD), f32),
            pltpu.VMEM((units, count, 4 * HD), f32),
            pltpu.VMEM((units, count, 2 * HD), f32),
            pltpu.VMEM((units, count, 2 * HD), f32),
            pltpu.VMEM((tpd, rows, 2 * HD), bf16),
            pltpu.VMEM((late, groups, rows, 2 * HD), bf16),
            pltpu.VMEM((groups, late * rows, 2 * HD), bf16),
            pltpu.SMEM((groups,), jnp.int32),
            dma, dma, dma((2,)), dma((2, 2)), dma((2,)),
            dma((2 * late,)), dma, dma((units,)), dma, dma, dma,
            dma, dma((units,)), dma, dma((units,)), dma, dma,
        ],
        compiler_params=pltpu.CompilerParams(
            collective_id=0, has_side_effects=True, vmem_limit_bytes=63 * 1024 * 1024
        ),
    )(image_feats.reshape(tpd, tile, feats), w_kv, k_gain.reshape(1, HD), tile_rows, deal.T)
    return (keys.reshape(tpd * tile, HD), values.reshape(tpd * tile, HD))


def build(mesh, nz, ny, tpd, tile, chunks, early=EARLY):
    placed = (P("gx", "gy"), P("gy", None), P(), P(), P())
    return jax.shard_map(
        functools.partial(local, nz, ny, tpd, tile, chunks, early),
        mesh=mesh, in_specs=placed, out_specs=(P("gx", "gy"), P("gx", "gy")), check_vma=False,
    )


def solution(mesh):
    return build(mesh, 8, 4, 16, 128, CHUNKS)
```

time: 108 us -> 85.7 us (0.79)
  Pallas kernels: 102 us -> 81.1 us
  local copies, waits for them, and re-layouts: 5.17 us -> 3.74 us
    pallas_call x1, Pallas kernels: 102 us -> 81.1 us  [local(): pl.pallas_call(functools.partial(kernel, nz, ny, tpd, tile, chunks, early...]
    unnamed x3 -> x2, local copies, waits for them, and re-layouts: 4.51 us -> 3.74 us
where the time goes in v3:
time: 85.7 us; the launch traced here: 85.5 us
  Pallas kernels  81.1 us (95%)
  local copies, waits for them, and re-layouts  3.74 us (4%)
    pallas_call x1, Pallas kernels, local(): pl.pallas_call(functools.partial(kernel, nz, ny, tpd, tile, chunks, early...  81.1 us
    unnamed x2, local copies, waits for them, and re-layouts  3.74 us

profile of v3, /device:TPU:1, one launch (start us, length us, event | category | flops | bytes accessed | tf_op | source)
XLA Modules:
  0.0 85.5 jit_solution(7454583894051894607)
XLA Ops:
  0.6 81.1 %shard_map.68 = (bf16[16,128,128]{2,1,0:T(8,128)(2,1)}, bf16[16,128,128]{2,1,0:T(8,128)(2,1)}) custom-call(bf16[16,128,512]{2,1,0:T(8,128)(2,1)} %bitcast.5, bf16[512,2048]{1,0:T(8,128)(2,1)} %w_ref.1, f32[1,128]{1,0:T(1,128)} %bitcast.9, s32[512]{0:T(512)} %rows_ref.1, s32[16,32]{1,0:T(8,128)} %bitcast.8), custom_call_target="tpu_custom_call" | custom-call | tf_op jit(solution)/shard_map/pallas_call | solution.py:281
  81.7 1.9 %copy.9 = bf16[2048,128]{1,0:T(8,128)(2,1)} copy(bf16[2048,128]{1,0:T(8,128)(2,1)} %bitcast.7) | data formatting | bytes 1048576
  83.6 1.9 %copy.10 = bf16[2048,128]{1,0:T(8,128)(2,1)} copy(bf16[2048,128]{1,0:T(8,128)(2,1)} %bitcast.6) | data formatting | bytes 1048576

commit v4 on v3

--- a/solution.py
+++ b/solution.py
@@ -24,8 +24,8 @@
 def kernel(
     nz, ny, tpd, tile, chunks, early,
     x_ref, w_ref, gain_ref, rows_ref, deal_ref, k_ref, v_ref,
-    wv, xo, xr, xf, xs, xd, keep, ps, pr, rs, rr, tiles, sb, rb, table,
-    w_local, w_send, w_mate, w_near, w_far, x_local, x_send, x_recv, f_local, f_send, f_recv,
+    wv, ws, xo, xr, xf, xs, xd, keep, ps, pr, rs, rr, tiles, sb, rb, table, rounds,
+    w_local, s_local, w_send, w_mate, w_y, w_z, x_local, x_send, x_recv, f_local, f_send, f_recv,
     p_send, p_recv, r_send, r_recv, d_send, d_recv,
 ):
     groups = nz * ny
@@ -35,6 +35,7 @@
     feats = x_ref.shape[2]
     total_kv = w_ref.shape[1] // 2
     tpu = tpd // 2
+    shift = tpd.bit_length() - 1
     count = tpu * rows
     units = 2 * chunks
     late_units = 2 * late
@@ -64,91 +65,105 @@
             src_ref=src, dst_ref=dst, send_sem=send, recv_sem=recv, device_id=device, device_id_type=MESH
         )
 
-    for block, owner in enumerate(owners(chip, core)):
+    colour = lax.rem(y + 2 * z, 4)
+    quarter = feats // 4
+    piece = quarter // 4
+    for block, (owner, sent) in enumerate(zip(owners(chip, core), owners(mate, core))):
         for part in range(2):
+            at = pl.ds((2 * block + part) * HD, HD)
             pltpu.make_async_copy(
-                w_ref.at[:, columns(owner, part)],
-                wv.at[pl.ds(0, feats), pl.ds((2 * block + part) * HD, HD)],
-                w_local,
+                w_ref.at[pl.ds(pl.multiple_of(colour * quarter, quarter), quarter), columns(sent, part)],
+                ws.at[:, at], s_local,
             ).start()
+            pltpu.make_async_copy(w_ref.at[:, columns(owner, part)], wv.at[pl.ds(0, feats), at], w_local).start()
     pltpu.make_async_copy(x_ref.at[:, pl.ds(late_rows, early_rows), :], xf, f_local).start()
     for u in range(late_units):
         pltpu.make_async_copy(
             x_ref.at[pl.ds(u % 2 * tpu, tpu), pl.ds(u // 2 * rows, rows), :], xo.at[u], x_local.at[u]
         ).start()
 
+    up_id, down_id = (peer(0, 1), gy), (peer(0, ny - 1), gy)
+    front_id, back_id = (peer(1, 0), gy), (peer(nz - 1, 0), gy)
     barrier = pltpu.get_barrier_semaphore()
     spread = offsets(nz, ny)
-    for device in (sibling_id, mate_id, across_id):
+    for device in (sibling_id, mate_id, across_id, up_id, down_id, front_id, back_id):
         pl.semaphore_signal(barrier, inc=1, device_id=device, device_id_type=MESH)
-    for dz, dy in spread:
-        pl.semaphore_signal(barrier, inc=1, device_id=(peer(dz, dy), gy), device_id_type=MESH)
+
+    def tell(number, pair):
+        for device in pair:
+            pl.semaphore_signal(rounds.at[number], inc=1, device_id=device, device_id_type=MESH)
+
+    def hear(number):
+        pl.semaphore_wait(rounds.at[number], 2)
 
     def find(d, carry):
         found = jnp.int32(0)
         for s in range(tpd):
-            source = lax.div(deal_ref[s, d], jnp.int32(tpd))
-            found = jnp.where(source == gx, s, found)
-        table[d] = found
+            source = lax.shift_right_logical(deal_ref[s, d], shift)
+            found = found + jnp.where(source == gx, s, 0)
+        table[d] = jnp.minimum(found, tpd - 1)
         return carry
-
-    lax.fori_loop(0, groups, find, 0)
-    pltpu.make_async_copy(x_ref.at[:, pl.ds(late_rows, early_rows), :], xf, f_local).wait()
 
     def gather(d, carry):
         xs[d] = xf[table[d]]
         return carry
 
-    lax.fori_loop(0, groups, gather, 0)
-    xd[gx] = xf[table[gx]]
-    pl.semaphore_wait(barrier, 3 + len(spread))
-
-    quarter = feats // ny
-    part_rows = quarter // 2
-
-    def share(owner_y, half):
-        at = pl.multiple_of(feats + owner_y * quarter + half * part_rows, part_rows)
-        return wv.at[pl.ds(at, part_rows), :]
-
-    for half in range(2):
-        source = pl.ds(pl.multiple_of(y * quarter + half * part_rows, part_rows), part_rows)
-        at = pl.ds(pl.multiple_of(feats + y * quarter + half * part_rows, part_rows), part_rows)
-        for block, owner in enumerate(owners(mate, core)):
-            for part in range(2):
-                remote(
-                    w_ref.at[source, columns(owner, part)],
-                    wv.at[at, pl.ds((2 * block + part) * HD, HD)],
-                    w_send, w_mate.at[half], mate_id,
-                ).start()
+    pltpu.make_async_copy(w_ref.at[pl.ds(0, quarter), pl.ds(0, 8 * HD)], ws, s_local).wait()
+    pl.semaphore_wait(barrier, 7)
+
+    def share(kind, start, size):
+        at = feats + lax.rem(kind, 4) * quarter + start * piece
+        return wv.at[pl.ds(pl.multiple_of(at, piece), size * piece), :]
+
+    for n in range(4):
+        remote(
+            ws.at[pl.ds(n * piece, piece), :], share(colour, n, 1), w_send, w_mate.at[n], mate_id
+        ).start()
     for u in range(late_units):
         remote(
             x_ref.at[pl.ds(u % 2 * tpu, tpu), pl.ds(u // 2 * rows, rows), :],
             xr.at[u], x_send, x_recv.at[u], mate_id,
         ).start()
+    tell(0, (front_id, back_id))
+    lax.fori_loop(0, groups, find, 0)
+    pltpu.make_async_copy(x_ref.at[:, pl.ds(late_rows, early_rows), :], xf, f_local).wait()
+    hear(0)
+    tell(1, (front_id, back_id))
+
+    def pass_on(n):
+        remote(share(colour, n, 1), share(colour, n, 1), w_send, w_mate.at[n], mate_id).wait_recv()
+        remote(share(colour, n, 1), share(colour, n, 1), w_send, w_y.at[0], up_id).start()
+        remote(share(colour, n, 1), share(colour, n, 1), w_send, w_y.at[1], down_id).start()
+        remote(
+            share(colour, n, 1), share(colour, n, 1), w_send, w_z.at[n // 2], front_id if n < 2 else back_id
+        ).start()
+
+    pass_on(0)
+    hear(1)
+    tell(2, (front_id, back_id))
+    lax.fori_loop(0, groups // 2, gather, 0)
+    pass_on(1)
+    hear(2)
+    tell(3, (up_id, down_id))
+    lax.fori_loop(groups // 2, groups, gather, 0)
+    xd[gx] = xf[table[gx]]
     for dz, dy in spread:
         if dy == 0:
             target = peer(dz, dy)
             remote(xs.at[target], xd.at[gx], f_send, f_recv, (target, gy)).start()
-
-    up, down = lax.rem(y + 1, ny), lax.rem(y + ny - 1, ny)
-    up_id, down_id = (z * ny + up, gy), (z * ny + down, gy)
-    for half in range(2):
-        remote(share(y, half), share(y, half), w_send, w_mate.at[half], mate_id).wait_recv()
-        remote(share(y, half), share(y, half), w_send, w_near.at[0, half], up_id).start()
-        remote(share(y, half), share(y, half), w_send, w_near.at[1, half], down_id).start()
-    remote(share(down, 0), share(down, 0), w_send, w_near.at[0, 0], up_id).wait_recv()
-    remote(share(down, 0), share(down, 0), w_send, w_far.at[0], up_id).start()
-    remote(share(up, 1), share(up, 1), w_send, w_near.at[1, 1], down_id).wait_recv()
-    remote(share(up, 1), share(up, 1), w_send, w_far.at[1], down_id).start()
+    pass_on(2)
+    hear(3)
+    tell(4, (up_id, down_id))
+    pass_on(3)
+    hear(4)
     for dz, dy in spread:
         if dy != 0:
             target = peer(dz, dy)
             remote(xs.at[target], xd.at[gx], f_send, f_recv, (target, gy)).start()
-    opposite = lax.rem(y + 2, ny)
-    remote(share(up, 0), share(up, 0), w_send, w_near.at[1, 0], down_id).wait_recv()
-    remote(share(down, 1), share(down, 1), w_send, w_near.at[0, 1], up_id).wait_recv()
-    remote(share(opposite, 0), share(opposite, 0), w_send, w_far.at[0], up_id).wait_recv()
-    remote(share(opposite, 1), share(opposite, 1), w_send, w_far.at[1], down_id).wait_recv()
+    remote(share(colour + 3, 0, 4), share(colour + 3, 0, 4), w_send, w_y.at[0], up_id).wait_recv()
+    remote(share(colour + 1, 0, 4), share(colour + 1, 0, 4), w_send, w_y.at[1], down_id).wait_recv()
+    remote(share(colour + 2, 0, 2), share(colour + 2, 0, 2), w_send, w_z.at[0], front_id).wait_recv()
+    remote(share(colour + 2, 2, 2), share(colour + 2, 2, 2), w_send, w_z.at[1], back_id).wait_recv()
     pltpu.make_async_copy(w_ref.at[:, pl.ds(0, 8 * HD)], wv.at[pl.ds(0, feats), :], w_local).wait()
 
     far = peer(*spread[0])
@@ -171,6 +186,8 @@
             )
             if part:
                 remote(ps.at[u], pr.at[u], p_send, p_recv.at[u], sibling_id).start()
+
+    def reduce(u):
         remote(ps.at[u], pr.at[u], p_send, p_recv.at[u], sibling_id).wait_recv()
         rs[u] = keep[u, :, 2 * HD:] + pr[u, :, 2 * HD:]
         remote(rs.at[u], rr.at[u], r_send, r_recv.at[u], across_id).start()
@@ -225,7 +242,7 @@
     def take_early():
         remote(xs.at[pl.ds(0, groups - 1)], xd.at[pl.ds(0, groups - 1)], f_send, f_recv, (far, gy)).wait_recv()
         for s in range(tpd):
-            source = lax.div(deal_ref[s, gx], jnp.int32(tpd))
+            source = lax.shift_right_logical(deal_ref[s, gx], shift)
             for e in range(early):
                 xo[late_units + 2 * e + s // tpu, s % tpu] = xd[source, e * rows:(e + 1) * rows, :]
         for u in range(late_units, units):
@@ -236,17 +253,21 @@
         def _():
             project(i)
 
+        @pl.when((i >= LAG) & (i < late_units + LAG))
+        def _():
+            finish_late(i - LAG)
+
+        @pl.when(i >= late_units + LAG)
+        def _():
+            finish_early(i - LAG)
+
+        @pl.when(i < units)
+        def _():
+            reduce(i)
+
         @pl.when(i == max(late_units - 3, 0))
         def _():
             take_early()
-
-        @pl.when((i >= LAG) & (i < late_units + LAG))
-        def _():
-            finish_late(i - LAG)
-
-        @pl.when(i >= late_units + LAG)
-        def _():
-            finish_early(i - LAG)
 
         return carry
 
@@ -254,7 +275,7 @@
 
     remote(sb.at[:, pl.ds(0, groups - 1)], rb.at[pl.ds(0, groups - 1)], d_send, d_recv, (far, gy)).wait_recv()
     for s in range(tpd):
-        source = lax.div(deal_ref[s, gx], jnp.int32(tpd))
+        source = lax.shift_right_logical(deal_ref[s, gx], shift)
         k_ref[s, 0:late_rows, :] = rb[source, :, :HD]
         v_ref[s, 0:late_rows, :] = rb[source, :, HD:]
 
@@ -285,6 +306,7 @@
         out_specs=(vmem, vmem),
         scratch_shapes=[
             pltpu.VMEM((2 * feats, 8 * HD), bf16),
+            pltpu.VMEM((feats // 4, 8 * HD), bf16),
             pltpu.VMEM((units, tpd // 2, rows, feats), bf16),
             pltpu.VMEM((units, tpd // 2, rows, feats), bf16),
             pltpu.VMEM((tpd, early * rows, feats), bf16),
@@ -299,7 +321,8 @@
             pltpu.VMEM((late, groups, rows, 2 * HD), bf16),
             pltpu.VMEM((groups, late * rows, 2 * HD), bf16),
             pltpu.SMEM((groups,), jnp.int32),
-            dma, dma, dma((2,)), dma((2, 2)), dma((2,)),
+            pltpu.SemaphoreType.REGULAR((5,)),
+            dma, dma, dma, dma((4,)), dma((2,)), dma((2,)),
             dma((2 * late,)), dma, dma((units,)), dma, dma, dma,
             dma, dma((units,)), dma, dma((units,)), dma, dma,
         ],

time: 85.7 us -> 82.7 us (0.965); the launches traced: 85.5 us -> 81.6 us
  Pallas kernels: 81.1 us -> 77.2 us
    pallas_call x1, Pallas kernels: 81.1 us -> 77.2 us  [local(): pl.pallas_call(functools.partial(kernel, nz, ny, tpd, tile, chunks, early...]
where the time goes in v4:
time: 82.7 us; the launch traced here: 81.6 us
  Pallas kernels  77.2 us (93%)
  local copies, waits for them, and re-layouts  3.74 us (5%)
    pallas_call x1, Pallas kernels, local(): pl.pallas_call(functools.partial(kernel, nz, ny, tpd, tile, chunks, early...  77.2 us
    unnamed x2, local copies, waits for them, and re-layouts  3.74 us

profile of v4, /device:TPU:1, one launch (start us, length us, event | category | flops | bytes accessed | tf_op | source)
XLA Modules:
  0.0 81.6 jit_solution(6553545675818586214)
XLA Ops:
  0.6 77.2 %shard_map.68 = (bf16[16,128,128]{2,1,0:T(8,128)(2,1)}, bf16[16,128,128]{2,1,0:T(8,128)(2,1)}) custom-call(bf16[16,128,512]{2,1,0:T(8,128)(2,1)} %bitcast.5, bf16[512,2048]{1,0:T(8,128)(2,1)} %w_ref.1, f32[1,128]{1,0:T(1,128)} %bitcast.9, s32[512]{0:T(512)} %rows_ref.1, s32[16,32]{1,0:T(8,128)} %bitcast.8), custom_call_target="tpu_custom_call" | custom-call | tf_op jit(solution)/shard_map/pallas_call | solution.py:302
  77.8 1.9 %copy.9 = bf16[2048,128]{1,0:T(8,128)(2,1)} copy(bf16[2048,128]{1,0:T(8,128)(2,1)} %bitcast.7) | data formatting | bytes 1048576
  79.7 1.9 %copy.10 = bf16[2048,128]{1,0:T(8,128)(2,1)} copy(bf16[2048,128]{1,0:T(8,128)(2,1)} %bitcast.6) | data formatting | bytes 1048576

commit v5 on v4

--- a/solution.py
+++ b/solution.py
@@ -23,7 +23,7 @@
 
 def kernel(
     nz, ny, tpd, tile, chunks, early,
-    x_ref, w_ref, gain_ref, rows_ref, deal_ref, k_ref, v_ref,
+    x_ref, w_ref, gain_ref, rows_ref, deal_ref, kv_ref,
     wv, ws, xo, xr, xf, xs, xd, keep, ps, pr, rs, rr, tiles, sb, rb, table, rounds,
     w_local, s_local, w_send, w_mate, w_y, w_z, x_local, x_send, x_recv, f_local, f_send, f_recv,
     p_send, p_recv, r_send, r_recv, d_send, d_recv,
@@ -147,19 +147,14 @@
     tell(3, (up_id, down_id))
     lax.fori_loop(groups // 2, groups, gather, 0)
     xd[gx] = xf[table[gx]]
-    for dz, dy in spread:
-        if dy == 0:
-            target = peer(dz, dy)
-            remote(xs.at[target], xd.at[gx], f_send, f_recv, (target, gy)).start()
     pass_on(2)
     hear(3)
     tell(4, (up_id, down_id))
     pass_on(3)
     hear(4)
     for dz, dy in spread:
-        if dy != 0:
-            target = peer(dz, dy)
-            remote(xs.at[target], xd.at[gx], f_send, f_recv, (target, gy)).start()
+        target = peer(dz, dy)
+        remote(xs.at[target], xd.at[gx], f_send, f_recv, (target, gy)).start()
     remote(share(colour + 3, 0, 4), share(colour + 3, 0, 4), w_send, w_y.at[0], up_id).wait_recv()
     remote(share(colour + 1, 0, 4), share(colour + 1, 0, 4), w_send, w_y.at[1], down_id).wait_recv()
     remote(share(colour + 2, 0, 2), share(colour + 2, 0, 2), w_send, w_z.at[0], front_id).wait_recv()
@@ -234,8 +229,8 @@
 
         def store(s, position, normed, value_pre):
             valid = position < rows_ref[deal_ref[s, gx]]
-            k_ref[s, place, :] = jnp.where(valid, normed, 0.0).astype(jnp.bfloat16)
-            v_ref[s, place, :] = jnp.where(valid, value_pre, 0.0).astype(jnp.bfloat16)
+            kv_ref[s, place, :HD] = jnp.where(valid, normed, 0.0).astype(jnp.bfloat16)
+            kv_ref[s, place, HD:] = jnp.where(valid, value_pre, 0.0).astype(jnp.bfloat16)
 
         normalize(u, store)
 
@@ -276,8 +271,7 @@
     remote(sb.at[:, pl.ds(0, groups - 1)], rb.at[pl.ds(0, groups - 1)], d_send, d_recv, (far, gy)).wait_recv()
     for s in range(tpd):
         source = lax.shift_right_logical(deal_ref[s, gx], shift)
-        k_ref[s, 0:late_rows, :] = rb[source, :, :HD]
-        v_ref[s, 0:late_rows, :] = rb[source, :, HD:]
+        kv_ref[s, 0:late_rows, :] = rb[source]
 
     remote(wv.at[pl.ds(0, feats), :], wv.at[pl.ds(0, feats), :], w_send, w_mate.at[0], mate_id).wait_send()
     remote(xo, xr, x_send, x_recv.at[0], mate_id).wait_send()
@@ -299,11 +293,11 @@
     any_space = pl.BlockSpec(memory_space=pltpu.HBM)
     vmem = pl.BlockSpec(memory_space=pltpu.VMEM)
     smem = pl.BlockSpec(memory_space=pltpu.SMEM)
-    keys, values = pl.pallas_call(
+    both = pl.pallas_call(
         functools.partial(kernel, nz, ny, tpd, tile, chunks, early),
-        out_shape=(jax.ShapeDtypeStruct((tpd, tile, HD), bf16),) * 2,
+        out_shape=jax.ShapeDtypeStruct((tpd, tile, 2 * HD), bf16),
         in_specs=[any_space, any_space, vmem, smem, smem],
-        out_specs=(vmem, vmem),
+        out_specs=vmem,
         scratch_shapes=[
             pltpu.VMEM((2 * feats, 8 * HD), bf16),
             pltpu.VMEM((feats // 4, 8 * HD), bf16),
@@ -330,7 +324,8 @@
             collective_id=0, has_side_effects=True, vmem_limit_bytes=63 * 1024 * 1024
         ),
     )(image_feats.reshape(tpd, tile, feats), w_kv, k_gain.reshape(1, HD), tile_rows, deal.T)
-    return (keys.reshape(tpd * tile, HD), values.reshape(tpd * tile, HD))
+    both = both.reshape(tpd * tile, 2 * HD)
+    return (both[:, :HD], both[:, HD:])
 
 
 def build(mesh, nz, ny, tpd, tile, chunks, early=EARLY):

time: 82.7 us -> 80.3 us (0.971); the launches traced: 81.6 us -> 80.1 us
  local copies, waits for them, and re-layouts: 3.74 us -> 2.24 us
    unnamed x2 -> x0, local copies, waits for them, and re-layouts: 3.74 us -> none
    slice x0 -> x1, local copies, waits for them, and re-layouts: none -> 2.24 us  [local(): return (both[:, :HD], both[:, HD:])]
where the time goes in v5:
time: 80.3 us; the launch traced here: 80.1 us
  Pallas kernels  77.2 us (96%)
  local copies, waits for them, and re-layouts  2.24 us (3%)
    pallas_call x1, Pallas kernels, local(): pl.pallas_call(functools.partial(kernel, nz, ny, tpd, tile, chunks, early...  77.2 us
    slice x1, local copies, waits for them, and re-layouts, local(): return (both[:, :HD], both[:, HD:])  2.24 us

profile of v5, /device:TPU:1, one launch (start us, length us, event | category | flops | bytes accessed | tf_op | source)
XLA Modules:
  0.0 80.1 jit_solution(8108241161525111295)
XLA Ops:
  0.6 77.2 %shard_map.68 = bf16[16,128,256]{2,1,0:T(8,128)(2,1)} custom-call(bf16[16,128,512]{2,1,0:T(8,128)(2,1)} %bitcast.5, bf16[512,2048]{1,0:T(8,128)(2,1)} %w_ref.1, f32[1,128]{1,0:T(1,128)} %bitcast.7, s32[512]{0:T(512)} %rows_ref.1, s32[16,32]{1,0:T(8,128)} %bitcast.6), custom_call_target="tpu_custom_call" | custom-call | tf_op jit(solution)/shard_map/pallas_call | solution.py:296
  77.9 2.2 %fusion = (bf16[2048,128]{1,0:T(8,128)(2,1)}, bf16[2048,128]{1,0:T(8,128)(2,1)}) fusion(bf16[2048,256]{1,0:T(8,128)(2,1)} %bitcast.4), kind=kLoop, calls=%fused_computation | loop fusion | bytes 2097152 | tf_op jit(solution)/shard_map/slice | solution.py:328

commit v6 on v5

--- a/solution.py
+++ b/solution.py
@@ -23,7 +23,7 @@
 
 def kernel(
     nz, ny, tpd, tile, chunks, early,
-    x_ref, w_ref, gain_ref, rows_ref, deal_ref, kv_ref,
+    x_ref, w_ref, gain_ref, deal_ref, kv_ref,
     wv, ws, xo, xr, xf, xs, xd, keep, ps, pr, rs, rr, tiles, sb, rb, table, rounds,
     w_local, s_local, w_send, w_mate, w_y, w_z, x_local, x_send, x_recv, f_local, f_send, f_recv,
     p_send, p_recv, r_send, r_recv, d_send, d_recv,
@@ -89,6 +89,9 @@
     for device in (sibling_id, mate_id, across_id, up_id, down_id, front_id, back_id):
         pl.semaphore_signal(barrier, inc=1, device_id=device, device_id_type=MESH)
 
+    def limit_of(t):
+        return deal_ref[tpd + lax.div(t, groups), lax.rem(t, groups)]
+
     def tell(number, pair):
         for device in pair:
             pl.semaphore_signal(rounds.at[number], inc=1, device_id=device, device_id_type=MESH)
@@ -151,10 +154,15 @@
     hear(3)
     tell(4, (up_id, down_id))
     pass_on(3)
+    for dz, dy in spread:
+        if dy == 0:
+            target = peer(dz, dy)
+            remote(xs.at[target], xd.at[gx], f_send, f_recv, (target, gy)).start()
     hear(4)
     for dz, dy in spread:
-        target = peer(dz, dy)
-        remote(xs.at[target], xd.at[gx], f_send, f_recv, (target, gy)).start()
+        if dy != 0:
+            target = peer(dz, dy)
+            remote(xs.at[target], xd.at[gx], f_send, f_recv, (target, gy)).start()
     remote(share(colour + 3, 0, 4), share(colour + 3, 0, 4), w_send, w_y.at[0], up_id).wait_recv()
     remote(share(colour + 1, 0, 4), share(colour + 1, 0, 4), w_send, w_y.at[1], down_id).wait_recv()
     remote(share(colour + 2, 0, 2), share(colour + 2, 0, 2), w_send, w_z.at[0], front_id).wait_recv()
@@ -205,7 +213,7 @@
         q = lax.div(u, 2)
 
         def store(s, position, normed, value_pre):
-            valid = position < rows_ref[gx * tpd + s]
+            valid = position < limit_of(gx * tpd + s)
             tiles[s, :, :HD] = jnp.where(valid, normed, 0.0).astype(jnp.bfloat16)
             tiles[s, :, HD:] = jnp.where(valid, value_pre, 0.0).astype(jnp.bfloat16)
 
@@ -228,7 +236,7 @@
         place = pl.ds(pl.multiple_of(lax.div(u, 2) * rows, rows), rows)
 
         def store(s, position, normed, value_pre):
-            valid = position < rows_ref[deal_ref[s, gx]]
+            valid = position < limit_of(deal_ref[s, gx])
             kv_ref[s, place, :HD] = jnp.where(valid, normed, 0.0).astype(jnp.bfloat16)
             kv_ref[s, place, HD:] = jnp.where(valid, value_pre, 0.0).astype(jnp.bfloat16)
 
@@ -296,7 +304,7 @@
     both = pl.pallas_call(
         functools.partial(kernel, nz, ny, tpd, tile, chunks, early),
         out_shape=jax.ShapeDtypeStruct((tpd, tile, 2 * HD), bf16),
-        in_specs=[any_space, any_space, vmem, smem, smem],
+        in_specs=[any_space, any_space, vmem, smem],
         out_specs=vmem,
         scratch_shapes=[
             pltpu.VMEM((2 * feats, 8 * HD), bf16),
@@ -321,9 +329,9 @@
             dma, dma((units,)), dma, dma((units,)), dma, dma,
         ],
         compiler_params=pltpu.CompilerParams(
-            collective_id=0, has_side_effects=True, vmem_limit_bytes=63 * 1024 * 1024
+            collective_id=0, has_side_effects=True, vmem_limit_bytes=51 * 1024 * 1024
         ),
-    )(image_feats.reshape(tpd, tile, feats), w_kv, k_gain.reshape(1, HD), tile_rows, deal.T)
+    )(image_feats.reshape(tpd, tile, feats), w_kv, k_gain.reshape(1, HD), jnp.concatenate([deal.T, tile_rows.reshape(tpd, groups)]))
     both = both.reshape(tpd * tile, 2 * HD)
     return (both[:, :HD], both[:, HD:])
 

time: 80.3 us -> 79.6 us (level)
  Pallas kernels: 77.2 us -> 74.8 us
    pallas_call x1, Pallas kernels: 77.2 us -> 74.8 us  [local(): pl.pallas_call(functools.partial(kernel, nz, ny, tpd, tile, chunks, early...]
    slice x1, local copies, waits for them, and re-layouts: 2.24 us -> 1.04 us  [local(): return (both[:, :HD], both[:, HD:])]
where the time goes in v6:
time: 79.6 us; the launch traced here: 78.6 us
  Pallas kernels  74.8 us (94%)
  local copies, waits for them, and re-layouts  2.45 us (3%)
    pallas_call x1, Pallas kernels, local(): pl.pallas_call(functools.partial(kernel, nz, ny, tpd, tile, chunks, early...  74.8 us

profile of v6, /device:TPU:1, one launch (start us, length us, event | category | flops | bytes accessed | tf_op | source)
XLA Modules:
  0.0 78.6 jit_solution(6314371014026359806)
XLA Ops:
  0.6 0.8 reshape.18
  1.4 0.7 pad_add_fusion.deal_ref
  2.1 0.0 copy-start
  2.1 0.7 copy-done
  2.7 74.8 %shard_map.68 = bf16[16,128,256]{2,1,0:T(8,128)(2,1)S(1)} custom-call(bf16[16,128,512]{2,1,0:T(8,128)(2,1)} %bitcast.6, bf16[512,2048]{1,0:T(8,128)(2,1)} %w_ref.1, f32[1,128]{1,0:T(1,128)S(1)} %bitcast.5, s32[32,32]{1,0:T(8,128)S(1)} %pad_add_fusion.deal_ref), custom_call_target="tpu_custom_call" | custom-call | tf_op jit(solution)/shard_map/pallas_call | solution.py:304
  77.6 1.0 %fusion = (bf16[2048,128]{1,0:T(8,128)(2,1)}, bf16[2048,128]{1,0:T(8,128)(2,1)}) fusion(bf16[2048,256]{1,0:T(8,128)(2,1)S(1)} %bitcast.4), kind=kLoop, calls=%fused_computation.1 | loop fusion | bytes 2097152 | tf_op jit(solution)/shard_map/slice | solution.py:336
Async XLA Ops:
  2.1 0.7 copy-start

commit v7 on v6

--- a/solution.py
+++ b/solution.py
@@ -67,7 +67,7 @@
 
     colour = lax.rem(y + 2 * z, 4)
     quarter = feats // 4
-    piece = quarter // 4
+    piece = quarter // 8
     for block, (owner, sent) in enumerate(zip(owners(chip, core), owners(mate, core))):
         for part in range(2):
             at = pl.ds((2 * block + part) * HD, HD)
@@ -118,7 +118,7 @@
         at = feats + lax.rem(kind, 4) * quarter + start * piece
         return wv.at[pl.ds(pl.multiple_of(at, piece), size * piece), :]
 
-    for n in range(4):
+    for n in range(8):
         remote(
             ws.at[pl.ds(n * piece, piece), :], share(colour, n, 1), w_send, w_mate.at[n], mate_id
         ).start()
@@ -138,22 +138,26 @@
         remote(share(colour, n, 1), share(colour, n, 1), w_send, w_y.at[0], up_id).start()
         remote(share(colour, n, 1), share(colour, n, 1), w_send, w_y.at[1], down_id).start()
         remote(
-            share(colour, n, 1), share(colour, n, 1), w_send, w_z.at[n // 2], front_id if n < 2 else back_id
+            share(colour, n, 1), share(colour, n, 1), w_send, w_z.at[n // 4], front_id if n < 4 else back_id
         ).start()
 
     pass_on(0)
+    pass_on(1)
     hear(1)
     tell(2, (front_id, back_id))
     lax.fori_loop(0, groups // 2, gather, 0)
-    pass_on(1)
+    pass_on(2)
+    pass_on(3)
     hear(2)
     tell(3, (up_id, down_id))
     lax.fori_loop(groups // 2, groups, gather, 0)
     xd[gx] = xf[table[gx]]
-    pass_on(2)
+    pass_on(4)
+    pass_on(5)
     hear(3)
     tell(4, (up_id, down_id))
-    pass_on(3)
+    pass_on(6)
+    pass_on(7)
     for dz, dy in spread:
         if dy == 0:
             target = peer(dz, dy)
@@ -163,10 +167,10 @@
         if dy != 0:
             target = peer(dz, dy)
             remote(xs.at[target], xd.at[gx], f_send, f_recv, (target, gy)).start()
-    remote(share(colour + 3, 0, 4), share(colour + 3, 0, 4), w_send, w_y.at[0], up_id).wait_recv()
-    remote(share(colour + 1, 0, 4), share(colour + 1, 0, 4), w_send, w_y.at[1], down_id).wait_recv()
-    remote(share(colour + 2, 0, 2), share(colour + 2, 0, 2), w_send, w_z.at[0], front_id).wait_recv()
-    remote(share(colour + 2, 2, 2), share(colour + 2, 2, 2), w_send, w_z.at[1], back_id).wait_recv()
+    remote(share(colour + 3, 0, 8), share(colour + 3, 0, 8), w_send, w_y.at[0], up_id).wait_recv()
+    remote(share(colour + 1, 0, 8), share(colour + 1, 0, 8), w_send, w_y.at[1], down_id).wait_recv()
+    remote(share(colour + 2, 0, 4), share(colour + 2, 0, 4), w_send, w_z.at[0], front_id).wait_recv()
+    remote(share(colour + 2, 4, 4), share(colour + 2, 4, 4), w_send, w_z.at[1], back_id).wait_recv()
     pltpu.make_async_copy(w_ref.at[:, pl.ds(0, 8 * HD)], wv.at[pl.ds(0, feats), :], w_local).wait()
 
     far = peer(*spread[0])
@@ -324,7 +328,7 @@
             pltpu.VMEM((groups, late * rows, 2 * HD), bf16),
             pltpu.SMEM((groups,), jnp.int32),
             pltpu.SemaphoreType.REGULAR((5,)),
-            dma, dma, dma, dma((4,)), dma((2,)), dma((2,)),
+            dma, dma, dma, dma((8,)), dma((2,)), dma((2,)),
             dma((2 * late,)), dma, dma((units,)), dma, dma, dma,
             dma, dma((units,)), dma, dma((units,)), dma, dma,
         ],

time: 79.6 us -> 79.2 us (level)
  no operation moved by 1% of the time
where the time goes in v7:
time: 79.2 us; the launch traced here: 78.6 us
  Pallas kernels  74.8 us (94%)
  local copies, waits for them, and re-layouts  2.45 us (3%)
    pallas_call x1, Pallas kernels, local(): pl.pallas_call(functools.partial(kernel, nz, ny, tpd, tile, chunks, early...  74.8 us

profile of v7, /device:TPU:1, one launch (start us, length us, event | category | flops | bytes accessed | tf_op | source)
XLA Modules:
  0.0 78.6 jit_solution(1493364695677267621)
XLA Ops:
  0.6 0.8 reshape.18
  1.4 0.7 pad_add_fusion.deal_ref
  2.1 0.0 copy-start
  2.1 0.7 copy-done
  2.7 74.8 %shard_map.68 = bf16[16,128,256]{2,1,0:T(8,128)(2,1)S(1)} custom-call(bf16[16,128,512]{2,1,0:T(8,128)(2,1)} %bitcast.6, bf16[512,2048]{1,0:T(8,128)(2,1)} %w_ref.1, f32[1,128]{1,0:T(1,128)S(1)} %bitcast.5, s32[32,32]{1,0:T(8,128)S(1)} %pad_add_fusion.deal_ref), custom_call_target="tpu_custom_call" | custom-call | tf_op jit(solution)/shard_map/pallas_call | solution.py:308
  77.6 1.0 %fusion = (bf16[2048,128]{1,0:T(8,128)(2,1)}, bf16[2048,128]{1,0:T(8,128)(2,1)}) fusion(bf16[2048,256]{1,0:T(8,128)(2,1)S(1)} %bitcast.4), kind=kLoop, calls=%fused_computation.1 | loop fusion | bytes 2097152 | tf_op jit(solution)/shard_map/slice | solution.py:340
Async XLA Ops:
  2.1 0.7 copy-start
